TPU v7x, 32 devices: a whole 2x2x4 slice. The times are simulated.
32 devices in a mesh: group: 4 (over y, x), shard: 8 (over z, core).
Axes of the slice: x: 2, y: 2, z: 4, core: 2. Of those that a mesh axis runs over, the one named last changes fastest.
Arguments:
- grad_pooled: bfloat16 [4096, 512, 128], P(('group', 'shard')), may hold values from -6 to 6
- bag_rows: int32 [4096, 512, 8], P(('group', 'shard')), may hold values from 0 to 511
- bag_lengths: int32 [4096, 512], P(('group', 'shard')), may hold values from 1 to 8
- table_order: int32 [512], replicated, may hold values from 0 to 511, each once
- weights: bfloat16 [512, 512, 128], P('shard'), may hold values from -6 to 6
- accum: float32 [512, 512], P('shard'), may hold values from 0.1 to 10
Outputs:
- new_weights: bfloat16 [512, 512, 128], P('shard')
- new_accum: float32 [512, 512], P('shard')
All inputs are finite; a program needn't handle non-finite values.
Results may differ from a plain program's by a relative error of at most 0.001.
Values may be sent and summed in bfloat16 or wider, within the bound.
A program may use at most 128 MiB of HBM per device.

v0:
```python
import jax
import jax.numpy as jnp
from jax import lax
from jax.sharding import PartitionSpec as P

LEARN_RATE = 0.5
EPSILON = 1e-06


def expand_rows(gradient, row_ids, row_count):
    tables_first = jnp.swapaxes(gradient, 0, 1)
    picks_first = jnp.transpose(row_ids, (1, 2, 0))

    def one_table(member):
        values, chosen = member
        positions = lax.broadcasted_iota(jnp.int32, (row_count, chosen.shape[1]), 0)
        counts = jnp.zeros((row_count, chosen.shape[1]), jnp.float32)
        for column in range(chosen.shape[0]):
            counts = counts + (chosen[column][None, :] == positions).astype(jnp.float32)
        return jnp.dot(counts.astype(jnp.bfloat16), values, preferred_element_type=jnp.float32)

    return lax.map(one_table, (tables_first, picks_first))


def adagrad(weight_rows, accum_rows, row_grad):
    new_accum = accum_rows + jnp.mean(row_grad * row_grad, axis=-1)
    step_size = LEARN_RATE / (jnp.sqrt(new_accum) + EPSILON)
    new_weights = (weight_rows.astype(jnp.float32) - step_size[:, :, None] * row_grad).astype(
        jnp.bfloat16
    )
    return (new_weights, new_accum)


def body(grad_pooled, bag_rows, bag_lengths, table_order, weights, accum):
    row_count = weights.shape[1]
    bag_size = bag_rows.shape[2]
    places = lax.broadcasted_iota(jnp.int32, bag_rows.shape, 2)
    live_rows = jnp.where(places < bag_lengths[:, :, None], bag_rows, -1)
    pooled = jnp.take(grad_pooled, table_order, axis=1)
    chosen = jnp.take(live_rows, table_order, axis=1)
    groups = lax.axis_size("group")
    shards = lax.axis_size("shard")
    quarter = weights.shape[0] // groups
    samples = pooled.shape[0]
    width = pooled.shape[2]
    pooled = pooled.reshape(samples, shards, groups, quarter, width)
    pooled = jnp.transpose(pooled, (0, 2, 1, 3, 4)).reshape(
        samples, shards * groups * quarter, width
    )
    chosen = chosen.reshape(samples, shards, groups, quarter, bag_size)
    chosen = jnp.transpose(chosen, (0, 2, 1, 3, 4)).reshape(
        samples, shards * groups * quarter, bag_size
    )
    gathered = lax.all_to_all(pooled, ("group", "shard"), split_axis=1, concat_axis=0, tiled=True)
    row_ids = lax.all_to_all(chosen, ("group", "shard"), split_axis=1, concat_axis=0, tiled=True)
    row_grad = expand_rows(gathered, row_ids, row_count)
    start = lax.axis_index("group") * quarter
    weight_part = lax.dynamic_slice_in_dim(weights, start, quarter, 0)
    accum_part = lax.dynamic_slice_in_dim(accum, start, quarter, 0)
    part_weights, part_accum = adagrad(weight_part, accum_part, row_grad)
    full_weights, full_accum = (
        lax.all_gather(part_weights.astype(jnp.float32), "group", axis=0, tiled=True),
        lax.all_gather(part_accum, "group", axis=0, tiled=True),
    )
    return (full_weights.astype(jnp.bfloat16), full_accum)


def solution(mesh):
    in_specs = (
        P(("group", "shard"), None, None),
        P(("group", "shard"), None, None),
        P(("group", "shard"), None),
        P(),
        P("shard", None, None),
        P("shard", None),
    )
    out_specs = (P("shard", None, None), P("shard", None))
    return jax.shard_map(body, mesh=mesh, in_specs=in_specs, out_specs=out_specs, check_vma=False)
```

profile of v0, /device:TPU:0, one launch (start us, length us, event | category | flops | bytes accessed | tf_op | source)
XLA Modules:
  0.0 827.4 jit_solution(13259575028350120470)
XLA Ops:
  7.2 0.7 compare_select_fusion
  7.8 0.7 compare_and_fusion
  8.5 0.1 broadcast_in_dim.38
  8.6 3.1 copy.22
  11.7 1.1 copy.21
  12.8 1.8 fusion.7
  14.6 2.7 gather_fusion
  17.3 1.9 select_bitcast_fusion
  19.3 1.5 copy.23
  20.7 7.3 all-to-all-start
  28.1 55.3 %gather_fusion.1 = bf16[512,128,128]{2,0,1:T(8,128)(2,1)} fusion(bf16[128,512,128]{2,1,0:T(8,128)(2,1)} %param.8, s32[1024]{0:T(1024)S(1)} %pad_clamp_fusion), kind=kCustom, calls=%fused_computation.1 | custom fusion | bytes 33556480 | tf_op jit(solution)/shard_map/jit(_take)/gather | solution.py:39
  83.4 9.1 %copy_select_fusion = bf16[128,8,4,16,128]{4,3,1,2,0:T(8,128)(2,1)S(1)} fusion(bf16[128,8,4,16,128]{4,3,2,1,0:T(8,128)(2,1)} %bitcast.64, pred[8,4,16]{2,0,1:T(8,128)(4,1)S(1)} %copy.25), kind=kLoop, calls=%fused_computation.25 | loop fusion | flops 8388608 | bytes 33554944 | tf_op jit(solution)/shard_map/jit(_take)/select_n | solution.py:39
  92.5 38.2 %copy.27 = bf16[128,512,128]{2,0,1:T(8,128)(2,1)} copy(bf16[128,512,128]{2,1,0:T(8,128)(2,1)S(1)} %bitcast.65) | data formatting | bytes 33554432 | tf_op jit(solution)/shard_map/reshape | solution.py:47
  130.6 0.0 all-to-all-done
  130.6 6.0 all-to-all-start.1
  136.6 0.0 all-gather.2.cloned.1.call-start
  136.7 1.5 copy.35
  138.2 362.9 %all-to-all-done.1 = bf16[128,512,128]{2,0,1:T(8,128)(2,1)} async-done(((bf16[128,512,128]{2,0,1:T(8,128)(2,1)}), bf16[128,512,128]{2,0,1:T(8,128)(2,1)}, u32[]{:S(2)}, u32[]{:S(2)}) %all-to-all-start.1) | async-done | bytes 16777248 | tf_op jit(solution)/shard_map/all_to_all | solution.py:54
  501.1 15.2 %copy.29 = bf16[32,128,16,128]{3,2,1,0:T(8,128)(2,1)S(1)} copy(bf16[32,128,16,128]{3,1,2,0:T(8,128)(2,1)} %bitcast.23) | data formatting | bytes 33554432 | tf_op jit(solution)/shard_map/all_to_all | solution.py:54
  516.4 11.9 %copy.30 = bf16[16,4096,128]{2,1,0:T(8,128)(2,1)} copy(bf16[16,4096,128]{2,0,1:T(8,128)(2,1)S(1)} %bitcast.66) | data formatting | bytes 33554432 | tf_op jit(solution)/shard_map/while | solution.py:22
  528.3 190.0 %while.10 = (s32[]{:T(128)}, f32[16,512,128]{2,1,0:T(8,128)}, s32[16,8,4096]{2,1,0:T(8,128)}, bf16[16,4096,128]{2,1,0:T(8,128)(2,1)}, s32[]{:T(128)}, /*index=5*...) while((s32[]{:T(128)}, f32[16,512,128]{2,1,0:T(8,128)}, s32[16,8,4096]{2,1,0:T(8,128)}, ...), condition=%wide.region_1.2_spmd, body=%wide.region_0.1_spmd.sunk | while | flops 587202560 | bytes 1705201 | solution.py:22
  528.3 1.6 constant_dynamic-slice_fusion.9
  529.9 10.2 %fusion.11 = f32[16,512,128]{2,1,0:T(8,128)} fusion(f32[16,512,128]{2,1,0:T(8,128)} %get-tuple-element.106, s32[]{:T(128)} %get-tuple-element.105, s32[4096]{0:T(1024)S(1)} %bitcast.77, s32[4096]{0:T(1024)S(1)} %bitcast.71, s32[4096]{0:T(1024)S(1)} %bitcast.72, s32[4096]{0:T(1024)S(1)} %bitcast.73, s32[4096]{0:T(1024)S(1)} %bitcast.74, ...), kind=kOutput, calls=%fused_computation.13.clone.1 | convolution fusion | flops 587202560 | bytes 1442816 | tf_op jit(solution)/shard_map/while/body/eval_jaxpr/dot_general | solution.py:20
  540.1 1.6 constant_dynamic-slice_fusion.9
  541.7 10.2 %fusion.11 = f32[16,512,128]{2,1,0:T(8,128)} fusion(f32[16,512,128]{2,1,0:T(8,128)} %get-tuple-element.106, s32[]{:T(128)} %get-tuple-element.105, s32[4096]{0:T(1024)S(1)} %bitcast.77, s32[4096]{0:T(1024)S(1)} %bitcast.71, s32[4096]{0:T(1024)S(1)} %bitcast.72, s32[4096]{0:T(1024)S(1)} %bitcast.73, s32[4096]{0:T(1024)S(1)} %bitcast.74, ...), kind=kOutput, calls=%fused_computation.13.clone.1 | convolution fusion | flops 587202560 | bytes 1442816 | tf_op jit(solution)/shard_map/while/body/eval_jaxpr/dot_general | solution.py:20
  551.9 1.9 constant_dynamic-slice_fusion.9
  553.8 10.2 %fusion.11 = f32[16,512,128]{2,1,0:T(8,128)} fusion(f32[16,512,128]{2,1,0:T(8,128)} %get-tuple-element.106, s32[]{:T(128)} %get-tuple-element.105, s32[4096]{0:T(1024)S(1)} %bitcast.77, s32[4096]{0:T(1024)S(1)} %bitcast.71, s32[4096]{0:T(1024)S(1)} %bitcast.72, s32[4096]{0:T(1024)S(1)} %bitcast.73, s32[4096]{0:T(1024)S(1)} %bitcast.74, ...), kind=kOutput, calls=%fused_computation.13.clone.1 | convolution fusion | flops 587202560 | bytes 1442816 | tf_op jit(solution)/shard_map/while/body/eval_jaxpr/dot_general | solution.py:20
  564.0 1.6 constant_dynamic-slice_fusion.9
  565.6 10.2 %fusion.11 = f32[16,512,128]{2,1,0:T(8,128)} fusion(f32[16,512,128]{2,1,0:T(8,128)} %get-tuple-element.106, s32[]{:T(128)} %get-tuple-element.105, s32[4096]{0:T(1024)S(1)} %bitcast.77, s32[4096]{0:T(1024)S(1)} %bitcast.71, s32[4096]{0:T(1024)S(1)} %bitcast.72, s32[4096]{0:T(1024)S(1)} %bitcast.73, s32[4096]{0:T(1024)S(1)} %bitcast.74, ...), kind=kOutput, calls=%fused_computation.13.clone.1 | convolution fusion | flops 587202560 | bytes 1442816 | tf_op jit(solution)/shard_map/while/body/eval_jaxpr/dot_general | solution.py:20
  575.8 1.6 constant_dynamic-slice_fusion.9
  577.4 10.2 %fusion.11 = f32[16,512,128]{2,1,0:T(8,128)} fusion(f32[16,512,128]{2,1,0:T(8,128)} %get-tuple-element.106, s32[]{:T(128)} %get-tuple-element.105, s32[4096]{0:T(1024)S(1)} %bitcast.77, s32[4096]{0:T(1024)S(1)} %bitcast.71, s32[4096]{0:T(1024)S(1)} %bitcast.72, s32[4096]{0:T(1024)S(1)} %bitcast.73, s32[4096]{0:T(1024)S(1)} %bitcast.74, ...), kind=kOutput, calls=%fused_computation.13.clone.1 | convolution fusion | flops 587202560 | bytes 1442816 | tf_op jit(solution)/shard_map/while/body/eval_jaxpr/dot_general | solution.py:20
  587.6 1.9 constant_dynamic-slice_fusion.9
  589.5 10.2 %fusion.11 = f32[16,512,128]{2,1,0:T(8,128)} fusion(f32[16,512,128]{2,1,0:T(8,128)} %get-tuple-element.106, s32[]{:T(128)} %get-tuple-element.105, s32[4096]{0:T(1024)S(1)} %bitcast.77, s32[4096]{0:T(1024)S(1)} %bitcast.71, s32[4096]{0:T(1024)S(1)} %bitcast.72, s32[4096]{0:T(1024)S(1)} %bitcast.73, s32[4096]{0:T(1024)S(1)} %bitcast.74, ...), kind=kOutput, calls=%fused_computation.13.clone.1 | convolution fusion | flops 587202560 | bytes 1442816 | tf_op jit(solution)/shard_map/while/body/eval_jaxpr/dot_general | solution.py:20
  599.7 1.6 constant_dynamic-slice_fusion.9
  601.3 10.2 %fusion.11 = f32[16,512,128]{2,1,0:T(8,128)} fusion(f32[16,512,128]{2,1,0:T(8,128)} %get-tuple-element.106, s32[]{:T(128)} %get-tuple-element.105, s32[4096]{0:T(1024)S(1)} %bitcast.77, s32[4096]{0:T(1024)S(1)} %bitcast.71, s32[4096]{0:T(1024)S(1)} %bitcast.72, s32[4096]{0:T(1024)S(1)} %bitcast.73, s32[4096]{0:T(1024)S(1)} %bitcast.74, ...), kind=kOutput, calls=%fused_computation.13.clone.1 | convolution fusion | flops 587202560 | bytes 1442816 | tf_op jit(solution)/shard_map/while/body/eval_jaxpr/dot_general | solution.py:20
  611.5 1.6 constant_dynamic-slice_fusion.9
  613.1 10.2 %fusion.11 = f32[16,512,128]{2,1,0:T(8,128)} fusion(f32[16,512,128]{2,1,0:T(8,128)} %get-tuple-element.106, s32[]{:T(128)} %get-tuple-element.105, s32[4096]{0:T(1024)S(1)} %bitcast.77, s32[4096]{0:T(1024)S(1)} %bitcast.71, s32[4096]{0:T(1024)S(1)} %bitcast.72, s32[4096]{0:T(1024)S(1)} %bitcast.73, s32[4096]{0:T(1024)S(1)} %bitcast.74, ...), kind=kOutput, calls=%fused_computation.13.clone.1 | convolution fusion | flops 587202560 | bytes 1442816 | tf_op jit(solution)/shard_map/while/body/eval_jaxpr/dot_general | solution.py:20
  623.3 1.9 constant_dynamic-slice_fusion.9
  625.1 10.2 %fusion.11 = f32[16,512,128]{2,1,0:T(8,128)} fusion(f32[16,512,128]{2,1,0:T(8,128)} %get-tuple-element.106, s32[]{:T(128)} %get-tuple-element.105, s32[4096]{0:T(1024)S(1)} %bitcast.77, s32[4096]{0:T(1024)S(1)} %bitcast.71, s32[4096]{0:T(1024)S(1)} %bitcast.72, s32[4096]{0:T(1024)S(1)} %bitcast.73, s32[4096]{0:T(1024)S(1)} %bitcast.74, ...), kind=kOutput, calls=%fused_computation.13.clone.1 | convolution fusion | flops 587202560 | bytes 1442816 | tf_op jit(solution)/shard_map/while/body/eval_jaxpr/dot_general | solution.py:20
  635.3 1.6 constant_dynamic-slice_fusion.9
  636.9 10.2 %fusion.11 = f32[16,512,128]{2,1,0:T(8,128)} fusion(f32[16,512,128]{2,1,0:T(8,128)} %get-tuple-element.106, s32[]{:T(128)} %get-tuple-element.105, s32[4096]{0:T(1024)S(1)} %bitcast.77, s32[4096]{0:T(1024)S(1)} %bitcast.71, s32[4096]{0:T(1024)S(1)} %bitcast.72, s32[4096]{0:T(1024)S(1)} %bitcast.73, s32[4096]{0:T(1024)S(1)} %bitcast.74, ...), kind=kOutput, calls=%fused_computation.13.clone.1 | convolution fusion | flops 587202560 | bytes 1442816 | tf_op jit(solution)/shard_map/while/body/eval_jaxpr/dot_general | solution.py:20
  647.1 1.6 constant_dynamic-slice_fusion.9
  648.7 10.2 %fusion.11 = f32[16,512,128]{2,1,0:T(8,128)} fusion(f32[16,512,128]{2,1,0:T(8,128)} %get-tuple-element.106, s32[]{:T(128)} %get-tuple-element.105, s32[4096]{0:T(1024)S(1)} %bitcast.77, s32[4096]{0:T(1024)S(1)} %bitcast.71, s32[4096]{0:T(1024)S(1)} %bitcast.72, s32[4096]{0:T(1024)S(1)} %bitcast.73, s32[4096]{0:T(1024)S(1)} %bitcast.74, ...), kind=kOutput, calls=%fused_computation.13.clone.1 | convolution fusion | flops 587202560 | bytes 1442816 | tf_op jit(solution)/shard_map/while/body/eval_jaxpr/dot_general | solution.py:20
  658.9 1.6 constant_dynamic-slice_fusion.9
  660.6 10.2 %fusion.11 = f32[16,512,128]{2,1,0:T(8,128)} fusion(f32[16,512,128]{2,1,0:T(8,128)} %get-tuple-element.106, s32[]{:T(128)} %get-tuple-element.105, s32[4096]{0:T(1024)S(1)} %bitcast.77, s32[4096]{0:T(1024)S(1)} %bitcast.71, s32[4096]{0:T(1024)S(1)} %bitcast.72, s32[4096]{0:T(1024)S(1)} %bitcast.73, s32[4096]{0:T(1024)S(1)} %bitcast.74, ...), kind=kOutput, calls=%fused_computation.13.clone.1 | convolution fusion | flops 587202560 | bytes 1442816 | tf_op jit(solution)/shard_map/while/body/eval_jaxpr/dot_general | solution.py:20
  670.7 1.6 constant_dynamic-slice_fusion.9
  672.4 10.2 %fusion.11 = f32[16,512,128]{2,1,0:T(8,128)} fusion(f32[16,512,128]{2,1,0:T(8,128)} %get-tuple-element.106, s32[]{:T(128)} %get-tuple-element.105, s32[4096]{0:T(1024)S(1)} %bitcast.77, s32[4096]{0:T(1024)S(1)} %bitcast.71, s32[4096]{0:T(1024)S(1)} %bitcast.72, s32[4096]{0:T(1024)S(1)} %bitcast.73, s32[4096]{0:T(1024)S(1)} %bitcast.74, ...), kind=kOutput, calls=%fused_computation.13.clone.1 | convolution fusion | flops 587202560 | bytes 1442816 | tf_op jit(solution)/shard_map/while/body/eval_jaxpr/dot_general | solution.py:20
  682.6 1.6 constant_dynamic-slice_fusion.9
  684.2 10.2 %fusion.11 = f32[16,512,128]{2,1,0:T(8,128)} fusion(f32[16,512,128]{2,1,0:T(8,128)} %get-tuple-element.106, s32[]{:T(128)} %get-tuple-element.105, s32[4096]{0:T(1024)S(1)} %bitcast.77, s32[4096]{0:T(1024)S(1)} %bitcast.71, s32[4096]{0:T(1024)S(1)} %bitcast.72, s32[4096]{0:T(1024)S(1)} %bitcast.73, s32[4096]{0:T(1024)S(1)} %bitcast.74, ...), kind=kOutput, calls=%fused_computation.13.clone.1 | convolution fusion | flops 587202560 | bytes 1442816 | tf_op jit(solution)/shard_map/while/body/eval_jaxpr/dot_general | solution.py:20
  694.4 1.9 constant_dynamic-slice_fusion.9
  696.3 10.2 %fusion.11 = f32[16,512,128]{2,1,0:T(8,128)} fusion(f32[16,512,128]{2,1,0:T(8,128)} %get-tuple-element.106, s32[]{:T(128)} %get-tuple-element.105, s32[4096]{0:T(1024)S(1)} %bitcast.77, s32[4096]{0:T(1024)S(1)} %bitcast.71, s32[4096]{0:T(1024)S(1)} %bitcast.72, s32[4096]{0:T(1024)S(1)} %bitcast.73, s32[4096]{0:T(1024)S(1)} %bitcast.74, ...), kind=kOutput, calls=%fused_computation.13.clone.1 | convolution fusion | flops 587202560 | bytes 1442816 | tf_op jit(solution)/shard_map/while/body/eval_jaxpr/dot_general | solution.py:20
  706.5 1.6 constant_dynamic-slice_fusion.9
  708.1 10.2 %fusion.11 = f32[16,512,128]{2,1,0:T(8,128)} fusion(f32[16,512,128]{2,1,0:T(8,128)} %get-tuple-element.106, s32[]{:T(128)} %get-tuple-element.105, s32[4096]{0:T(1024)S(1)} %bitcast.77, s32[4096]{0:T(1024)S(1)} %bitcast.71, s32[4096]{0:T(1024)S(1)} %bitcast.72, s32[4096]{0:T(1024)S(1)} %bitcast.73, s32[4096]{0:T(1024)S(1)} %bitcast.74, ...), kind=kOutput, calls=%fused_computation.13.clone.1 | convolution fusion | flops 587202560 | bytes 1442816 | tf_op jit(solution)/shard_map/while/body/eval_jaxpr/dot_general | solution.py:20
  718.3 3.3 multiply_reduce_fusion
  721.6 0.8 add_divide_fusion
  722.4 4.4 fusion.6
  726.8 0.0 all-gather.2.cloned.1.call-update
  726.8 7.5 all_gather.7
  734.3 77.8 %all-gather.2.cloned.1.call-done = bf16[64,512,128]{2,1,0:T(8,128)(2,1)} async-done(((bf16[16,512,128]{2,1,0:T(8,128)(2,1)}), bf16[64,512,128]{2,1,0:T(8,128)(2,1)}) %all-gather.2.cloned.1.call-update) | async-done | bytes 8388624 | tf_op jit(solution)/shard_map/all_gather | solution.py:62
  812.1 7.8 copy.45
  819.9 0.7 copy.46
  (3 shorter events, 0.0 us)
Async XLA Ops:
  20.7 109.9 %all-to-all-start = ((s32[128,512,8]{0,2,1:T(8,128)}), s32[128,512,8]{0,2,1:T(8,128)S(1)}, u32[]{:S(2)}, u32[]{:S(2)}) async-start(s32[128,512,8]{0,2,1:T(8,128)} %bitcast.68), calls=%async_computation | async-start | bytes 4194304 | tf_op jit(solution)/shard_map/all_to_all | solution.py:55
  130.6 370.5 %all-to-all-start.1 = ((bf16[128,512,128]{2,0,1:T(8,128)(2,1)}), bf16[128,512,128]{2,0,1:T(8,128)(2,1)}, u32[]{:S(2)}, u32[]{:S(2)}) async-start(bf16[128,512,128]{2,0,1:T(8,128)(2,1)} %copy.27), calls=%async_computation.1 | async-start | bytes 33554432 | tf_op jit(solution)/shard_map/all_to_all | solution.py:54
  136.6 675.5 %all-gather.2.cloned.1.call-start = ((), (), s32[]{:S(2)}) async-start(), calls=%async_computation.2 | async-start | bytes 10485760 | tf_op jit(solution)/shard_map/all_gather | solution.py:62
Sparse Core Ops, SparseCore 0:
  727.0 85.1 all-gather.1
where the time goes:
time: 829 us; the launch traced here: 827 us
  waiting for transfers between devices  441 us (53%)
  local copies, waits for them, and re-layouts  166 us (20%)
  matrix products  163 us (20%)
  other arithmetic  22.7 us (3%)
  between operations  14.1 us (2%)
  starting transfers between devices  13.3 us (2%)
    all_to_all x1, waiting for transfers between devices, body(): lax.all_to_all(pooled, ('group', 'shard'), split_axis=1, concat_axis=0, t...  363 us
    dot_general x16, matrix products, one_table(): jnp.dot(counts.astype(jnp.bfloat16), values, preferred_element_type=jnp.f...  163 us
    all_gather x1, waiting for transfers between devices, body(): lax.all_gather(part_weights.astype(jnp.float32), 'group', axis=0, tiled=T...  77.8 us
    gather x1, local copies, waits for them, and re-layouts, body(): pooled = jnp.take(grad_pooled, table_order, axis=1)  55.3 us
    reshape x1, local copies, waits for them, and re-layouts, body(): jnp.transpose(pooled, (0, 2, 1, 3, 4))  38.2 us
    slice x16, local copies, waits for them, and re-layouts, one_table(): counts = counts + (chosen[column][None, :] == positions).astype(jnp.float32)  26.8 us
  transfers between devices with their start and end apart: 3, of which 2 were waited for; matrix products, arithmetic and copies ran while one was open for 13% of the time, Pallas kernels for 0%

commit v1 on v0

--- a/solution.py
+++ b/solution.py
@@ -51,7 +51,10 @@
     chosen = jnp.transpose(chosen, (0, 2, 1, 3, 4)).reshape(
         samples, shards * groups * quarter, bag_size
     )
-    gathered = lax.all_to_all(pooled, ("group", "shard"), split_axis=1, concat_axis=0, tiled=True)
+    size = lax.axis_size(("group", "shard"))
+    blocks = jnp.stack(jnp.split(pooled, size, axis=1), axis=0)
+    blocks = lax.all_to_all(blocks, ("group", "shard"), split_axis=0, concat_axis=0)
+    gathered = jnp.concatenate(blocks, axis=0)
     row_ids = lax.all_to_all(chosen, ("group", "shard"), split_axis=1, concat_axis=0, tiled=True)
     row_grad = expand_rows(gathered, row_ids, row_count)
     start = lax.axis_index("group") * quarter

time: 829 us -> 807 us (0.973)
  local copies, waits for them, and re-layouts: 166 us -> 144 us
    unnamed x4 -> x35, local copies, waits for them, and re-layouts: 12.6 us -> 39.7 us
    reshape x1, local copies, waits for them, and re-layouts: 38.2 us -> 15.1 us  [body(): gathered = jnp.concatenate(blocks, axis=0)]
    all_to_all x1 -> x0, local copies, waits for them, and re-layouts: 15.2 us -> none  [body(): lax.all_to_all(pooled, ('group', 'shard'), split_axis=1, concat_axis=0, t...]
    while x1 -> x0, local copies, waits for them, and re-layouts: 11.9 us -> none  [expand_rows(): return lax.map(one_table, (tables_first, picks_first))]
  transfers between devices with their start and end apart: 3 -> 3, of which waited for: 2 -> 2; matrix products, arithmetic and copies ran while one was open for 13% -> 12% of each run, Pallas kernels for 0% -> 0%
where the time goes in v1:
time: 807 us; the launch traced here: 805 us
  waiting for transfers between devices  441 us (55%)
  matrix products  163 us (20%)
  local copies, waits for them, and re-layouts  144 us (18%)
  other arithmetic  22.9 us (3%)
  between operations  14.1 us (2%)
  starting transfers between devices  13.3 us (2%)
    all_to_all x1, waiting for transfers between devices, body(): lax.all_to_all(blocks, ('group', 'shard'), split_axis=0, concat_axis=0)  363 us
    dot_general x16, matrix products, one_table(): jnp.dot(counts.astype(jnp.bfloat16), values, preferred_element_type=jnp.f...  163 us
    all_gather x1, waiting for transfers between devices, body(): lax.all_gather(part_weights.astype(jnp.float32), 'group', axis=0, tiled=T...  77.8 us
    gather x1, local copies, waits for them, and re-layouts, body(): pooled = jnp.take(grad_pooled, table_order, axis=1)  55.3 us
    unnamed x35, local copies, waits for them, and re-layouts  39.7 us
    slice x16, local copies, waits for them, and re-layouts, one_table(): counts = counts + (chosen[column][None, :] == positions).astype(jnp.float32)  26.8 us
  transfers between devices with their start and end apart: 3, of which 2 were waited for; matrix products, arithmetic and copies ran while one was open for 12% of the time, Pallas kernels for 0%

profile of v1, /device:TPU:0, one launch (start us, length us, event | category | flops | bytes accessed | tf_op | source)
XLA Modules:
  0.0 805.4 jit_solution(18384485396412939239)
XLA Ops:
  8.6 3.1 copy.82
  11.7 1.1 copy.81
  12.8 1.8 fusion.7
  14.6 2.7 gather_fusion
  17.3 1.9 select_bitcast_fusion
  19.3 1.5 copy.83
  20.7 7.3 all-to-all-start
  28.1 55.3 %gather_fusion.1 = bf16[512,128,128]{2,0,1:T(8,128)(2,1)} fusion(bf16[128,512,128]{2,1,0:T(8,128)(2,1)} %param.8, s32[1024]{0:T(1024)S(1)} %pad_clamp_fusion), kind=kCustom, calls=%fused_computation.1 | custom fusion | bytes 33556480 | tf_op jit(solution)/shard_map/jit(_take)/gather | solution.py:39
  83.4 9.3 %copy_select_fusion = bf16[128,8,4,16,128]{4,3,1,2,0:T(8,128)(2,1)S(1)} fusion(bf16[128,8,4,16,128]{4,3,2,1,0:T(8,128)(2,1)} %bitcast.222, pred[8,4,16]{2,0,1:T(8,128)(4,1)S(1)} %copy.85), kind=kLoop, calls=%fused_computation.26 | loop fusion | flops 8388608 | bytes 33554944 | tf_op jit(solution)/shard_map/jit(_take)/select_n | solution.py:39
  94.4 0.9 fusion.37
  97.0 0.9 fusion.34
  101.3 0.9 fusion.29
  103.1 0.9 fusion.27
  105.7 0.9 fusion.24
  106.6 0.9 fusion.23
  107.5 0.9 fusion.22
  110.1 0.9 fusion.19
  112.8 0.9 fusion.16
  113.6 0.9 fusion.15
  114.5 0.9 fusion.14
  117.2 0.9 fusion.11
  119.8 0.9 fusion.8
  120.7 6.0 all-to-all-start.1
  126.7 1.5 copy.93
  128.2 362.9 %all-to-all-done.1 = bf16[32,128,16,128]{3,2,1,0:T(8,128)(2,1)} async-done(((bf16[32,128,16,128]{3,2,1,0:T(8,128)(2,1)}), bf16[32,128,16,128]{3,2,1,0:T(8,128)(2,1)}, u32[]{:S(2)}, u32[]{:S(2)}) %all-to-all-start.1) | async-done | bytes 16777248 | tf_op jit(solution)/shard_map/all_to_all | solution.py:56
  491.2 15.1 %copy.92 = bf16[4096,16,128]{2,0,1:T(8,128)(2,1)} copy(bf16[4096,16,128]{2,1,0:T(8,128)(2,1)} %bitcast.54) | data formatting | bytes 33554432 | tf_op jit(solution)/shard_map/reshape | solution.py:57
  506.3 190.0 %while.10 = (s32[]{:T(128)}, f32[16,512,128]{2,1,0:T(8,128)}, s32[16,8,4096]{2,1,0:T(8,128)}, bf16[16,4096,128]{2,1,0:T(8,128)(2,1)}, s32[]{:T(128)}, /*index=5*...) while((s32[]{:T(128)}, f32[16,512,128]{2,1,0:T(8,128)}, s32[16,8,4096]{2,1,0:T(8,128)}, ...), condition=%wide.region_1.2_spmd, body=%wide.region_0.1_spmd.sunk | while | flops 587202560 | bytes 1705201 | solution.py:22
  506.3 1.6 constant_dynamic-slice_fusion.9
  507.9 10.2 %fusion.43 = f32[16,512,128]{2,1,0:T(8,128)} fusion(f32[16,512,128]{2,1,0:T(8,128)} %get-tuple-element.98, s32[]{:T(128)} %get-tuple-element.97, s32[4096]{0:T(1024)S(1)} %bitcast.234, s32[4096]{0:T(1024)S(1)} %bitcast.228, s32[4096]{0:T(1024)S(1)} %bitcast.229, s32[4096]{0:T(1024)S(1)} %bitcast.230, s32[4096]{0:T(1024)S(1)} %bitcast.231, ...), kind=kOutput, calls=%fused_computation.13.clone.1 | convolution fusion | flops 587202560 | bytes 1442816 | tf_op jit(solution)/shard_map/while/body/eval_jaxpr/dot_general | solution.py:20
  518.1 1.6 constant_dynamic-slice_fusion.9
  519.7 10.2 %fusion.43 = f32[16,512,128]{2,1,0:T(8,128)} fusion(f32[16,512,128]{2,1,0:T(8,128)} %get-tuple-element.98, s32[]{:T(128)} %get-tuple-element.97, s32[4096]{0:T(1024)S(1)} %bitcast.234, s32[4096]{0:T(1024)S(1)} %bitcast.228, s32[4096]{0:T(1024)S(1)} %bitcast.229, s32[4096]{0:T(1024)S(1)} %bitcast.230, s32[4096]{0:T(1024)S(1)} %bitcast.231, ...), kind=kOutput, calls=%fused_computation.13.clone.1 | convolution fusion | flops 587202560 | bytes 1442816 | tf_op jit(solution)/shard_map/while/body/eval_jaxpr/dot_general | solution.py:20
  529.9 1.9 constant_dynamic-slice_fusion.9
  531.8 10.2 %fusion.43 = f32[16,512,128]{2,1,0:T(8,128)} fusion(f32[16,512,128]{2,1,0:T(8,128)} %get-tuple-element.98, s32[]{:T(128)} %get-tuple-element.97, s32[4096]{0:T(1024)S(1)} %bitcast.234, s32[4096]{0:T(1024)S(1)} %bitcast.228, s32[4096]{0:T(1024)S(1)} %bitcast.229, s32[4096]{0:T(1024)S(1)} %bitcast.230, s32[4096]{0:T(1024)S(1)} %bitcast.231, ...), kind=kOutput, calls=%fused_computation.13.clone.1 | convolution fusion | flops 587202560 | bytes 1442816 | tf_op jit(solution)/shard_map/while/body/eval_jaxpr/dot_general | solution.py:20
  542.0 1.6 constant_dynamic-slice_fusion.9
  543.6 10.2 %fusion.43 = f32[16,512,128]{2,1,0:T(8,128)} fusion(f32[16,512,128]{2,1,0:T(8,128)} %get-tuple-element.98, s32[]{:T(128)} %get-tuple-element.97, s32[4096]{0:T(1024)S(1)} %bitcast.234, s32[4096]{0:T(1024)S(1)} %bitcast.228, s32[4096]{0:T(1024)S(1)} %bitcast.229, s32[4096]{0:T(1024)S(1)} %bitcast.230, s32[4096]{0:T(1024)S(1)} %bitcast.231, ...), kind=kOutput, calls=%fused_computation.13.clone.1 | convolution fusion | flops 587202560 | bytes 1442816 | tf_op jit(solution)/shard_map/while/body/eval_jaxpr/dot_general | solution.py:20
  553.8 1.6 constant_dynamic-slice_fusion.9
  555.4 10.2 %fusion.43 = f32[16,512,128]{2,1,0:T(8,128)} fusion(f32[16,512,128]{2,1,0:T(8,128)} %get-tuple-element.98, s32[]{:T(128)} %get-tuple-element.97, s32[4096]{0:T(1024)S(1)} %bitcast.234, s32[4096]{0:T(1024)S(1)} %bitcast.228, s32[4096]{0:T(1024)S(1)} %bitcast.229, s32[4096]{0:T(1024)S(1)} %bitcast.230, s32[4096]{0:T(1024)S(1)} %bitcast.231, ...), kind=kOutput, calls=%fused_computation.13.clone.1 | convolution fusion | flops 587202560 | bytes 1442816 | tf_op jit(solution)/shard_map/while/body/eval_jaxpr/dot_general | solution.py:20
  565.6 1.9 constant_dynamic-slice_fusion.9
  567.4 10.2 %fusion.43 = f32[16,512,128]{2,1,0:T(8,128)} fusion(f32[16,512,128]{2,1,0:T(8,128)} %get-tuple-element.98, s32[]{:T(128)} %get-tuple-element.97, s32[4096]{0:T(1024)S(1)} %bitcast.234, s32[4096]{0:T(1024)S(1)} %bitcast.228, s32[4096]{0:T(1024)S(1)} %bitcast.229, s32[4096]{0:T(1024)S(1)} %bitcast.230, s32[4096]{0:T(1024)S(1)} %bitcast.231, ...), kind=kOutput, calls=%fused_computation.13.clone.1 | convolution fusion | flops 587202560 | bytes 1442816 | tf_op jit(solution)/shard_map/while/body/eval_jaxpr/dot_general | solution.py:20
  577.6 1.6 constant_dynamic-slice_fusion.9
  579.2 10.2 %fusion.43 = f32[16,512,128]{2,1,0:T(8,128)} fusion(f32[16,512,128]{2,1,0:T(8,128)} %get-tuple-element.98, s32[]{:T(128)} %get-tuple-element.97, s32[4096]{0:T(1024)S(1)} %bitcast.234, s32[4096]{0:T(1024)S(1)} %bitcast.228, s32[4096]{0:T(1024)S(1)} %bitcast.229, s32[4096]{0:T(1024)S(1)} %bitcast.230, s32[4096]{0:T(1024)S(1)} %bitcast.231, ...), kind=kOutput, calls=%fused_computation.13.clone.1 | convolution fusion | flops 587202560 | bytes 1442816 | tf_op jit(solution)/shard_map/while/body/eval_jaxpr/dot_general | solution.py:20
  589.4 1.6 constant_dynamic-slice_fusion.9
  591.1 10.2 %fusion.43 = f32[16,512,128]{2,1,0:T(8,128)} fusion(f32[16,512,128]{2,1,0:T(8,128)} %get-tuple-element.98, s32[]{:T(128)} %get-tuple-element.97, s32[4096]{0:T(1024)S(1)} %bitcast.234, s32[4096]{0:T(1024)S(1)} %bitcast.228, s32[4096]{0:T(1024)S(1)} %bitcast.229, s32[4096]{0:T(1024)S(1)} %bitcast.230, s32[4096]{0:T(1024)S(1)} %bitcast.231, ...), kind=kOutput, calls=%fused_computation.13.clone.1 | convolution fusion | flops 587202560 | bytes 1442816 | tf_op jit(solution)/shard_map/while/body/eval_jaxpr/dot_general | solution.py:20
  601.2 1.9 constant_dynamic-slice_fusion.9
  603.1 10.2 %fusion.43 = f32[16,512,128]{2,1,0:T(8,128)} fusion(f32[16,512,128]{2,1,0:T(8,128)} %get-tuple-element.98, s32[]{:T(128)} %get-tuple-element.97, s32[4096]{0:T(1024)S(1)} %bitcast.234, s32[4096]{0:T(1024)S(1)} %bitcast.228, s32[4096]{0:T(1024)S(1)} %bitcast.229, s32[4096]{0:T(1024)S(1)} %bitcast.230, s32[4096]{0:T(1024)S(1)} %bitcast.231, ...), kind=kOutput, calls=%fused_computation.13.clone.1 | convolution fusion | flops 587202560 | bytes 1442816 | tf_op jit(solution)/shard_map/while/body/eval_jaxpr/dot_general | solution.py:20
  613.3 1.6 constant_dynamic-slice_fusion.9
  614.9 10.2 %fusion.43 = f32[16,512,128]{2,1,0:T(8,128)} fusion(f32[16,512,128]{2,1,0:T(8,128)} %get-tuple-element.98, s32[]{:T(128)} %get-tuple-element.97, s32[4096]{0:T(1024)S(1)} %bitcast.234, s32[4096]{0:T(1024)S(1)} %bitcast.228, s32[4096]{0:T(1024)S(1)} %bitcast.229, s32[4096]{0:T(1024)S(1)} %bitcast.230, s32[4096]{0:T(1024)S(1)} %bitcast.231, ...), kind=kOutput, calls=%fused_computation.13.clone.1 | convolution fusion | flops 587202560 | bytes 1442816 | tf_op jit(solution)/shard_map/while/body/eval_jaxpr/dot_general | solution.py:20
  625.1 1.6 constant_dynamic-slice_fusion.9
  626.7 10.2 %fusion.43 = f32[16,512,128]{2,1,0:T(8,128)} fusion(f32[16,512,128]{2,1,0:T(8,128)} %get-tuple-element.98, s32[]{:T(128)} %get-tuple-element.97, s32[4096]{0:T(1024)S(1)} %bitcast.234, s32[4096]{0:T(1024)S(1)} %bitcast.228, s32[4096]{0:T(1024)S(1)} %bitcast.229, s32[4096]{0:T(1024)S(1)} %bitcast.230, s32[4096]{0:T(1024)S(1)} %bitcast.231, ...), kind=kOutput, calls=%fused_computation.13.clone.1 | convolution fusion | flops 587202560 | bytes 1442816 | tf_op jit(solution)/shard_map/while/body/eval_jaxpr/dot_general | solution.py:20
  636.9 1.6 constant_dynamic-slice_fusion.9
  638.5 10.2 %fusion.43 = f32[16,512,128]{2,1,0:T(8,128)} fusion(f32[16,512,128]{2,1,0:T(8,128)} %get-tuple-element.98, s32[]{:T(128)} %get-tuple-element.97, s32[4096]{0:T(1024)S(1)} %bitcast.234, s32[4096]{0:T(1024)S(1)} %bitcast.228, s32[4096]{0:T(1024)S(1)} %bitcast.229, s32[4096]{0:T(1024)S(1)} %bitcast.230, s32[4096]{0:T(1024)S(1)} %bitcast.231, ...), kind=kOutput, calls=%fused_computation.13.clone.1 | convolution fusion | flops 587202560 | bytes 1442816 | tf_op jit(solution)/shard_map/while/body/eval_jaxpr/dot_general | solution.py:20
  648.7 1.6 constant_dynamic-slice_fusion.9
  650.3 10.2 %fusion.43 = f32[16,512,128]{2,1,0:T(8,128)} fusion(f32[16,512,128]{2,1,0:T(8,128)} %get-tuple-element.98, s32[]{:T(128)} %get-tuple-element.97, s32[4096]{0:T(1024)S(1)} %bitcast.234, s32[4096]{0:T(1024)S(1)} %bitcast.228, s32[4096]{0:T(1024)S(1)} %bitcast.229, s32[4096]{0:T(1024)S(1)} %bitcast.230, s32[4096]{0:T(1024)S(1)} %bitcast.231, ...), kind=kOutput, calls=%fused_computation.13.clone.1 | convolution fusion | flops 587202560 | bytes 1442816 | tf_op jit(solution)/shard_map/while/body/eval_jaxpr/dot_general | solution.py:20
  660.5 1.6 constant_dynamic-slice_fusion.9
  662.1 10.2 %fusion.43 = f32[16,512,128]{2,1,0:T(8,128)} fusion(f32[16,512,128]{2,1,0:T(8,128)} %get-tuple-element.98, s32[]{:T(128)} %get-tuple-element.97, s32[4096]{0:T(1024)S(1)} %bitcast.234, s32[4096]{0:T(1024)S(1)} %bitcast.228, s32[4096]{0:T(1024)S(1)} %bitcast.229, s32[4096]{0:T(1024)S(1)} %bitcast.230, s32[4096]{0:T(1024)S(1)} %bitcast.231, ...), kind=kOutput, calls=%fused_computation.13.clone.1 | convolution fusion | flops 587202560 | bytes 1442816 | tf_op jit(solution)/shard_map/while/body/eval_jaxpr/dot_general | solution.py:20
  672.3 1.9 constant_dynamic-slice_fusion.9
  674.2 10.2 %fusion.43 = f32[16,512,128]{2,1,0:T(8,128)} fusion(f32[16,512,128]{2,1,0:T(8,128)} %get-tuple-element.98, s32[]{:T(128)} %get-tuple-element.97, s32[4096]{0:T(1024)S(1)} %bitcast.234, s32[4096]{0:T(1024)S(1)} %bitcast.228, s32[4096]{0:T(1024)S(1)} %bitcast.229, s32[4096]{0:T(1024)S(1)} %bitcast.230, s32[4096]{0:T(1024)S(1)} %bitcast.231, ...), kind=kOutput, calls=%fused_computation.13.clone.1 | convolution fusion | flops 587202560 | bytes 1442816 | tf_op jit(solution)/shard_map/while/body/eval_jaxpr/dot_general | solution.py:20
  684.4 1.6 constant_dynamic-slice_fusion.9
  686.1 10.2 %fusion.43 = f32[16,512,128]{2,1,0:T(8,128)} fusion(f32[16,512,128]{2,1,0:T(8,128)} %get-tuple-element.98, s32[]{:T(128)} %get-tuple-element.97, s32[4096]{0:T(1024)S(1)} %bitcast.234, s32[4096]{0:T(1024)S(1)} %bitcast.228, s32[4096]{0:T(1024)S(1)} %bitcast.229, s32[4096]{0:T(1024)S(1)} %bitcast.230, s32[4096]{0:T(1024)S(1)} %bitcast.231, ...), kind=kOutput, calls=%fused_computation.13.clone.1 | convolution fusion | flops 587202560 | bytes 1442816 | tf_op jit(solution)/shard_map/while/body/eval_jaxpr/dot_general | solution.py:20
  696.2 3.3 multiply_reduce_fusion
  700.4 4.4 fusion.6
  704.8 7.5 all_gather.7
  712.3 77.8 %all-gather.2.cloned.1.call-done = bf16[64,512,128]{2,1,0:T(8,128)(2,1)} async-done(((bf16[16,512,128]{2,1,0:T(8,128)(2,1)}), bf16[64,512,128]{2,1,0:T(8,128)(2,1)}) %all-gather.2.cloned.1.call-update) | async-done | bytes 8388624 | tf_op jit(solution)/shard_map/all_gather | solution.py:65
  790.1 7.8 copy.134
  (30 shorter events, 19.4 us)
Async XLA Ops:
  20.7 99.9 %all-to-all-start = ((s32[128,512,8]{0,2,1:T(8,128)}), s32[128,512,8]{0,2,1:T(8,128)S(1)}, u32[]{:S(2)}, u32[]{:S(2)}) async-start(s32[128,512,8]{0,2,1:T(8,128)} %bitcast.225), calls=%async_computation | async-start | bytes 4194304 | tf_op jit(solution)/shard_map/all_to_all | solution.py:58
  120.7 370.5 %all-to-all-start.1 = ((bf16[32,128,16,128]{3,2,1,0:T(8,128)(2,1)}), bf16[32,128,16,128]{3,2,1,0:T(8,128)(2,1)}, u32[]{:S(2)}, u32[]{:S(2)}) async-start(bf16[32,128,16,128]{3,2,1,0:T(8,128)(2,1)} %fusion.8), calls=%async_computation.1 | async-start | bytes 33554432 | tf_op jit(solution)/shard_map/all_to_all | solution.py:56
  126.6 663.5 %all-gather.2.cloned.1.call-start = ((), (), s32[]{:S(2)}) async-start(), calls=%async_computation.2 | async-start | bytes 10485760 | tf_op jit(solution)/shard_map/all_gather | solution.py:65
Sparse Core Ops, SparseCore 0:
  704.9 85.1 all-gather.1
